TPU v7x, 32 devices: a whole 2x2x4 slice. The times are simulated.
32 devices in a mesh: wide: 8 (over y, x, core), narrow: 4 (over z).
Axes of the slice: x: 2, y: 2, z: 4, core: 2. Of those that a mesh axis runs over, the one named last changes fastest.
Arguments:
- tokens: bfloat16 [8192, 2048], P(('wide', 'narrow')), may hold values from -6 to 6
- out_grad: bfloat16 [8192, 2048], P(('wide', 'narrow')), may hold values from -6 to 6
- captions: bfloat16 [4096, 4096], P(('wide', 'narrow')), may hold values from -6 to 6
- image_blocks: int32 [32, 256], P('wide'), may hold values from 0 to 3, never falling along the last dimension, each value on 1 to 128 neighbouring positions
- caption_owner: int32 [8, 512], P('wide'), may hold values from 0 to 3, never falling along the last dimension, each value on 1 to 256 neighbouring positions
- norm_gains: float32 [3, 2048], replicated, may hold values from 0.25 to 1.75
- norm_shifts: float32 [3, 2048], replicated, may hold values from -3 to 3
- w_query: float32 [2048, 2048], P('wide', 'narrow'), may hold values from -0.125 to 0.125
- w_key: float32 [2048, 2048], P('wide', 'narrow'), may hold values from -0.125 to 0.125
- w_value: float32 [2048, 2048], P('wide', 'narrow'), may hold values from -0.125 to 0.125
- w_out: float32 [2048, 2048], P('narrow', 'wide'), may hold values from -0.375 to 0.375
- w_cross_query: float32 [2048, 2048], P('wide', 'narrow'), may hold values from -0.125 to 0.125
- w_cross_key: float32 [4096, 2048], P('wide', 'narrow'), may hold values from -0.09375 to 0.09375
- w_cross_value: float32 [4096, 2048], P('wide', 'narrow'), may hold values from -0.09375 to 0.09375
- w_cross_out: float32 [2048, 2048], P('narrow', 'wide'), may hold values from -0.375 to 0.375
- w_up: float32 [2048, 8192], P('wide', 'narrow'), may hold values from -0.125 to 0.125
- w_down: float32 [8192, 2048], P('narrow', 'wide'), may hold values from -0.0625 to 0.0625
Outputs:
- block_out: bfloat16 [8192, 2048], P(('wide', 'narrow'))
- grad_tokens: bfloat16 [8192, 2048], P(('wide', 'narrow'))
- grad_captions: bfloat16 [4096, 4096], P(('wide', 'narrow'))
- grad_norm_gains: float32 [3, 2048], replicated
- grad_norm_shifts: float32 [3, 2048], replicated
- grad_w_query: float32 [2048, 2048], P('wide', 'narrow')
- grad_w_key: float32 [2048, 2048], P('wide', 'narrow')
- grad_w_value: float32 [2048, 2048], P('wide', 'narrow')
- grad_w_out: float32 [2048, 2048], P('narrow', 'wide')
- grad_w_cross_query: float32 [2048, 2048], P('wide', 'narrow')
- grad_w_cross_key: float32 [4096, 2048], P('wide', 'narrow')
- grad_w_cross_value: float32 [4096, 2048], P('wide', 'narrow')
- grad_w_cross_out: float32 [2048, 2048], P('narrow', 'wide')
- grad_w_up: float32 [2048, 8192], P('wide', 'narrow')
- grad_w_down: float32 [8192, 2048], P('narrow', 'wide')
Inputs may be any that keep to these rules, and one draw needn't show every extreme that they name: `image_blocks`: within an image the block numbers never fall; each of the 4 blocks has 1 to 128 tokens, and one block of every image has exactly that many. `caption_owner`: within a group the owners never fall; every image of the group has 1 to 256 caption tokens, and one image of every group has exactly 256.
All inputs are finite; a program needn't handle non-finite values.
Results may differ from a plain program's by a relative error of at most 0.024.
Values may be sent and summed in bfloat16 or wider, within the bound.
A program may use at most 320 MiB of HBM per device.

v0:
```python
import jax
import jax.numpy as jnp
from jax import lax
from jax.sharding import PartitionSpec as P

HEAD_DIM = 128
PIX = 256
CHUNKS = 2
EPSILON = 1e-06
MASKED = -1000000000.0
BF = jnp.bfloat16
F32 = jnp.float32


def product(left_side, right_side):
    return lax.dot_general(
        left_side, right_side, (((left_side.ndim - 1,), (0,)), ((), ())), preferred_element_type=F32
    )


def right_inner(left_side, right_side):
    return lax.dot_general(
        left_side, right_side, (((left_side.ndim - 1,), (1,)), ((), ())), preferred_element_type=F32
    )


def left_inner(left_side, right_side):
    rows = tuple(range(left_side.ndim - 1))
    return lax.dot_general(
        left_side, right_side, ((rows, rows), ((), ())), preferred_element_type=F32
    )


def spread(rows):
    n = lax.axis_size("narrow")
    here = lax.axis_index("narrow")
    up, down = ([rows], [rows])
    for step in range(1, n):
        up.append(lax.ppermute(up[-1], "narrow", [(k, k + 1) for k in range(step - 1, n - 1)]))
        down.append(lax.ppermute(down[-1], "narrow", [(k, k - 1) for k in range(1, n - step + 1)]))
    parts = [rows] + [jnp.where(here >= s, up[s], down[n - s]) for s in range(1, n)]
    return jnp.stack(parts)


def sink(parts):
    n = lax.axis_size("narrow")
    up = down = None
    for step in range(1, n):
        one, other = (parts[step], parts[n - step])
        if up is not None:
            one = up.astype(F32) + one.astype(F32)
            other = down.astype(F32) + other.astype(F32)
        up = lax.ppermute(one.astype(BF), "narrow", [(k, k + 1) for k in range(step)])
        down = lax.ppermute(other.astype(BF), "narrow", [(k, k - 1) for k in range(n - step, n)])
    return up.astype(F32) + down.astype(F32) + parts[0].astype(F32)


def norm_stats(features):
    center = features - jnp.mean(features, axis=-1, keepdims=True)
    rstd = lax.rsqrt(jnp.mean(center * center, axis=-1, keepdims=True) + EPSILON)
    return (center * rstd, rstd)


def norm_back(grad, xhat, rstd, gain):
    scaled = grad * gain
    return rstd * (
        scaled
        - jnp.mean(scaled, axis=-1, keepdims=True)
        - xhat * jnp.mean(scaled * xhat, axis=-1, keepdims=True)
    )


def norm_sums(grad, xhat):
    return jnp.stack([jnp.sum(grad * xhat, axis=0), jnp.sum(grad, axis=0)])


def score_block(queries, keys_in, allowed, score_scale):
    raw = jnp.einsum("iphe,iqhe->ihpq", queries, keys_in, preferred_element_type=F32)
    return jnp.where(allowed[:, None], raw * score_scale, MASKED)


def attend(queries, keys_in, values_in, allowed, score_scale):
    scores = score_block(queries, keys_in, allowed, score_scale)
    log_total = jax.nn.logsumexp(scores, axis=-1, keepdims=True)
    soft = jnp.exp(scores - log_total).astype(BF)
    mixture = jnp.einsum("ihpq,iqhe->iphe", soft, values_in, preferred_element_type=F32)
    return (mixture.astype(BF), log_total)


def attend_back(queries, keys_in, values_in, allowed, log_total, grad_mix, score_scale):
    soft = jnp.exp(score_block(queries, keys_in, allowed, score_scale) - log_total)
    grad_soft = jnp.einsum("iphe,iqhe->ihpq", grad_mix, values_in, preferred_element_type=F32)
    grad_values = jnp.einsum(
        "ihpq,iphe->iqhe", soft.astype(BF), grad_mix, preferred_element_type=F32
    )
    row_dot = jnp.sum(soft * grad_soft, axis=-1, keepdims=True)
    grad_scores = (soft * (grad_soft - row_dot) * score_scale).astype(BF)
    grad_queries = jnp.einsum("ihpq,iqhe->iphe", grad_scores, keys_in, preferred_element_type=F32)
    grad_keys = jnp.einsum("ihpq,iphe->iqhe", grad_scores, queries, preferred_element_type=F32)
    return (grad_queries.astype(BF), grad_keys, grad_values)


def after(value, *others):
    return lax.optimization_barrier((value, *others))[0]


def follow(value, other):
    return value + (other[(0,) * other.ndim].astype(F32) * 0.0).astype(value.dtype)


def exchange_sum(value):
    for axis in ("wide", "narrow"):
        size = lax.axis_size(axis)
        step = 1
        while step < size:
            value = value + lax.ppermute(value, axis, [(k, k ^ step) for k in range(size)])
            step *= 2
    return value


def body(
    tokens,
    out_grad,
    captions,
    image_blocks,
    caption_owner,
    norm_gains,
    norm_shifts,
    w_query,
    w_key,
    w_value,
    w_out,
    w_cross_query,
    w_cross_key,
    w_cross_value,
    w_cross_out,
    w_up,
    w_down,
):
    scale = HEAD_DIM ** (-0.5)
    n = lax.axis_size("narrow")
    here = lax.axis_index("narrow")
    width = w_query.shape[1]
    heads = width // HEAD_DIM
    part = PIX // CHUNKS
    chunks = [slice(c * part, (c + 1) * part) for c in range(CHUNKS)]
    image_of = (here - jnp.arange(n)) % n

    def relative(blocks):
        return jnp.stack(
            [lax.dynamic_index_in_dim(blocks, image_of[s], 0, False) for s in range(n)]
        )

    def rows_of(*pieces):
        return lax.all_gather(
            jnp.concatenate([p.astype(BF) for p in pieces], axis=1), "wide", axis=0, tiled=True
        )

    def columns_of(piece):
        return lax.all_gather(piece.astype(BF), "wide", axis=1, tiled=True)

    def to_rows(g):
        return lax.psum_scatter(g.astype(BF), "wide", scatter_dimension=0, tiled=True).astype(F32)

    def to_columns(g):
        return lax.psum_scatter(g.astype(BF), "wide", scatter_dimension=1, tiled=True).astype(F32)

    full_qkv = rows_of(w_query, w_key, w_value)
    full_out = columns_of(w_out)
    full_ckv = rows_of(w_cross_key, w_cross_value)
    full_cq = rows_of(w_cross_query)
    full_cout = columns_of(w_cross_out)
    full_up = rows_of(w_up)
    full_down = columns_of(w_down)
    residual0 = tokens.astype(F32)
    xhat1, rstd1 = norm_stats(residual0)
    own1 = (xhat1 * norm_gains[0] + norm_shifts[0]).astype(BF)
    normed1 = spread(own1)
    qkv = product(normed1, full_qkv).astype(BF)
    heads_of = lambda x: x.reshape(x.shape[:-1] + (x.shape[-1] // HEAD_DIM, HEAD_DIM))
    self_q, self_k, self_v = [heads_of(qkv[..., k * width : (k + 1) * width]) for k in range(3)]
    blocks = image_blocks[image_of]
    self_allowed = blocks[:, :, None] == blocks[:, None, :]
    self_mix, self_total = attend(self_q, self_k, self_v, self_allowed, scale)
    self_mix = self_mix.reshape(n, PIX, width)
    text_rows = lax.all_gather(captions, "narrow", axis=0, tiled=True)
    text_count, text_width = text_rows.shape
    ckv = product(text_rows, full_ckv).astype(BF)
    cross_k = heads_of(ckv[None, :, :width])
    cross_v = heads_of(ckv[None, :, width:])
    owner = caption_owner[0]
    part_image = jnp.repeat(image_of, part)
    cross_allowed = (part_image[:, None] == owner[None, :])[None]
    state = []
    for rows in chunks:
        residual1 = residual0[rows] + sink(product(self_mix[:, rows], full_out).astype(BF))
        xhat2, rstd2 = norm_stats(residual1)
        state.append((residual1, xhat2, rstd2))
    normed2 = [spread((s[1] * norm_gains[1] + norm_shifts[1]).astype(BF)) for s in state]
    grad_all = relative(lax.all_gather(out_grad, "narrow", axis=0))
    cross_q, cross_mix, cross_total, state3 = ([], [], [], [])
    for c in range(CHUNKS):
        q = heads_of(product(normed2[c], full_cq).astype(BF).reshape(1, n * part, width))
        mix, total = attend(q, cross_k, cross_v, cross_allowed, scale)
        mix = mix.reshape(n, part, width)
        residual2 = state[c][0] + sink(product(mix, full_cout).astype(BF))
        xhat3, rstd3 = norm_stats(residual2)
        cross_q.append(q)
        cross_mix.append(mix)
        cross_total.append(total)
        state3.append((residual2, xhat3, rstd3))
    normed3 = [spread((s[1] * norm_gains[2] + norm_shifts[2]).astype(BF)) for s in state3]
    out_parts, acts, grad_hiddens, grad2, sums3 = ([], [], [], [], [])
    for c, rows in enumerate(chunks):
        if c > 0:
            normed3[c] = follow(normed3[c], sent)
        hidden = product(normed3[c], full_up)
        grad_rows = grad_all[:, rows]
        acted, gelu_back = jax.vjp(jax.nn.gelu, hidden)
        acted = acted.astype(BF)
        grad_hidden = gelu_back(right_inner(grad_rows, full_down))[0].astype(BF)
        acts.append(acted)
        grad_hiddens.append(grad_hidden)
        sent = lax.optimization_barrier(right_inner(grad_hidden, full_up).astype(BF))
        grad_n3 = sink(sent)
        residual2, xhat3, rstd3 = state3[c]
        sums3.append(norm_sums(grad_n3, xhat3))
        grad2.append(out_grad[rows].astype(F32) + norm_back(grad_n3, xhat3, rstd3, norm_gains[2]))
        out_parts.append(product(acted, full_down).astype(BF))
    cat = lambda xs: jnp.concatenate(xs, axis=1)
    acted, grad_hidden, n3 = (cat(acts), cat(grad_hiddens), cat(normed3))
    grad_down = left_inner(acted, cat([grad_all[:, rows] for rows in chunks]))
    grad_up = left_inner(n3, grad_hidden)
    out_sum = lax.psum_scatter(relative(cat(out_parts)), "narrow", scatter_dimension=0)
    block_out = (jnp.concatenate([s[0] for s in state3]) + out_sum.astype(F32)).astype(BF)
    e2 = [spread(g.astype(BF)) for g in grad2]
    own_down = to_columns(grad_down)
    own_up = to_rows(grad_up)
    e2[-1] = after(e2[-1], grad_down, grad_up)
    grad1, sums2, grad_cqs, grad_ck, grad_cv = ([], [], [], 0.0, 0.0)
    for c in range(CHUNKS):
        grad_mix = heads_of(right_inner(e2[c], full_cout).astype(BF).reshape(1, n * part, width))
        gq, gk, gv = attend_back(
            cross_q[c], cross_k, cross_v, cross_allowed, cross_total[c], grad_mix, scale
        )
        gq = gq.reshape(n, part, width)
        grad_cqs.append(gq)
        grad_ck = grad_ck + gk
        grad_cv = grad_cv + gv
        grad_n2 = sink(right_inner(gq, full_cq).astype(BF))
        _, xhat2, rstd2 = state[c]
        sums2.append(norm_sums(grad_n2, xhat2))
        grad1.append(grad2[c] + norm_back(grad_n2, xhat2, rstd2, norm_gains[1]))
    grad_cout = left_inner(cat(cross_mix), cat(e2))
    grad_cq = left_inner(cat(normed2), cat(grad_cqs))
    grad_ckv = jnp.concatenate(
        [grad_ck.reshape(text_count, width), grad_cv.reshape(text_count, width)], axis=1
    ).astype(BF)
    grad_text_part = right_inner(grad_ckv, full_ckv).astype(BF).reshape(n, -1, text_width)
    grad_wckv = left_inner(text_rows, grad_ckv)
    e1 = [spread(g.astype(BF)) for g in grad1]
    own_cout = to_columns(grad_cout)
    own_cq = to_rows(grad_cq)
    own_ckv = to_rows(grad_wckv)
    e1[-1] = after(e1[-1], grad_cout, grad_cq, grad_wckv, grad_text_part)
    grad_mix = heads_of(cat([right_inner(e, full_out).astype(BF) for e in e1]))
    grad_mix = after(grad_mix, own_down, own_up)
    gq, gk, gv = attend_back(self_q, self_k, self_v, self_allowed, self_total, grad_mix, scale)
    grad_qkv = jnp.concatenate([g.astype(BF).reshape(n, PIX, width) for g in (gq, gk, gv)], axis=-1)
    grad_out = left_inner(self_mix, cat(e1))
    grad_wqkv = left_inner(normed1, grad_qkv)
    grad_n1 = sink(right_inner(after(grad_qkv, grad_wqkv), full_qkv).astype(BF))
    grad_text = sink(relative(after(grad_text_part, grad_mix))).astype(BF)
    grad1 = jnp.concatenate(grad1)
    grad_n1 = after(grad_n1, own_cout, own_cq, own_ckv)
    grad_tokens = (grad1 + norm_back(grad_n1, xhat1, rstd1, norm_gains[0])).astype(BF)
    sums = exchange_sum(jnp.stack([norm_sums(grad_n1, xhat1), sum(sums2), sum(sums3)]))
    own_out = to_columns(grad_out)
    own_qkv = to_rows(grad_wqkv)
    return (
        block_out,
        grad_tokens,
        grad_text,
        sums[:, 0],
        sums[:, 1],
        own_qkv[:, :width],
        own_qkv[:, width : 2 * width],
        own_qkv[:, 2 * width :],
        own_out,
        own_cq,
        own_ckv[:, :width],
        own_ckv[:, width:],
        own_cout,
        own_up,
        own_down,
    )


def solution(mesh):
    in_specs = (
        P(("wide", "narrow"), None),
        P(("wide", "narrow"), None),
        P(("wide", "narrow"), None),
        P("wide", None),
        P("wide", None),
        P(),
        P(),
        P("wide", "narrow"),
        P("wide", "narrow"),
        P("wide", "narrow"),
        P("narrow", "wide"),
        P("wide", "narrow"),
        P("wide", "narrow"),
        P("wide", "narrow"),
        P("narrow", "wide"),
        P("wide", "narrow"),
        P("narrow", "wide"),
    )
    out_specs = (
        P(("wide", "narrow"), None),
        P(("wide", "narrow"), None),
        P(("wide", "narrow"), None),
        P(),
        P(),
        P("wide", "narrow"),
        P("wide", "narrow"),
        P("wide", "narrow"),
        P("narrow", "wide"),
        P("wide", "narrow"),
        P("wide", "narrow"),
        P("wide", "narrow"),
        P("narrow", "wide"),
        P("wide", "narrow"),
        P("narrow", "wide"),
    )
    return jax.shard_map(body, mesh=mesh, in_specs=in_specs, out_specs=out_specs, check_vma=False)
```

profile of v0, /device:TPU:0, one launch (start us, length us, event | category | flops | bytes accessed | tf_op | source)
XLA Modules:
  0.0 1377.7 jit_solution(2369147938922174307)
XLA Ops:
  28.0 21.0 %collective-permute-done = bf16[256,2048]{1,0:T(8,128)(2,1)S(1)} collective-permute-done((bf16[256,2048]{1,0:T(8,128)(2,1)S(1)}, bf16[256,2048]{1,0:T(8,128)(2,1)S(1)}, u32[]{:S(2)}, u32[]{:S(2)}) %collective-permute-start) | collective-permute-done | bytes 1048608 | tf_op jit(solution)/shard_map/ppermute | solution.py:39
  57.5 22.6 %collective-permute-done.2 = bf16[256,2048]{1,0:T(8,128)(2,1)} collective-permute-done((bf16[256,2048]{1,0:T(8,128)(2,1)S(1)}, bf16[256,2048]{1,0:T(8,128)(2,1)}, u32[]{:S(2)}, u32[]{:S(2)}) %collective-permute-start.2) | collective-permute-done | bytes 1048608 | tf_op jit(solution)/shard_map/ppermute | solution.py:40
  85.7 19.9 %collective-permute-done.3 = bf16[256,2048]{1,0:T(8,128)(2,1)S(1)} collective-permute-done((bf16[256,2048]{1,0:T(8,128)(2,1)}, bf16[256,2048]{1,0:T(8,128)(2,1)S(1)}, u32[]{:S(2)}, u32[]{:S(2)}) %collective-permute-start.3) | collective-permute-done | bytes 1048608 | tf_op jit(solution)/shard_map/ppermute | solution.py:40
  133.5 18.8 %collective-permute-done.6 = bf16[128,2048]{1,0:T(8,128)(2,1)S(1)} collective-permute-done((bf16[128,2048]{1,0:T(8,128)(2,1)S(1)}, bf16[128,2048]{1,0:T(8,128)(2,1)S(1)}, u32[]{:S(2)}, u32[]{:S(2)}) %collective-permute-start.6) | collective-permute-done | bytes 524320 | tf_op jit(solution)/shard_map/ppermute | solution.py:53
  157.7 17.1 %collective-permute-done.24 = bf16[128,2048]{1,0:T(8,128)(2,1)S(1)} collective-permute-done((bf16[128,2048]{1,0:T(8,128)(2,1)S(1)}, bf16[128,2048]{1,0:T(8,128)(2,1)S(1)}, u32[]{:S(2)}, u32[]{:S(2)}) %collective-permute-start.24) | collective-permute-done | bytes 524320 | tf_op jit(solution)/shard_map/ppermute | solution.py:53
  180.2 17.0 %collective-permute-done.7 = bf16[128,2048]{1,0:T(8,128)(2,1)S(1)} collective-permute-done((bf16[128,2048]{1,0:T(8,128)(2,1)S(1)}, bf16[128,2048]{1,0:T(8,128)(2,1)S(1)}, u32[]{:S(2)}, u32[]{:S(2)}) %collective-permute-start.7) | collective-permute-done | bytes 524320 | tf_op jit(solution)/shard_map/ppermute | solution.py:53
  203.4 16.4 %collective-permute-done.25 = bf16[128,2048]{1,0:T(8,128)(2,1)S(1)} collective-permute-done((bf16[128,2048]{1,0:T(8,128)(2,1)S(1)}, bf16[128,2048]{1,0:T(8,128)(2,1)S(1)}, u32[]{:S(2)}, u32[]{:S(2)}) %collective-permute-start.25) | collective-permute-done | bytes 524320 | tf_op jit(solution)/shard_map/ppermute | solution.py:53
  226.3 15.9 %collective-permute-done.8 = bf16[128,2048]{1,0:T(8,128)(2,1)S(1)} collective-permute-done((bf16[128,2048]{1,0:T(8,128)(2,1)S(1)}, bf16[128,2048]{1,0:T(8,128)(2,1)S(1)}, u32[]{:S(2)}, u32[]{:S(2)}) %collective-permute-start.8) | collective-permute-done | bytes 524320 | tf_op jit(solution)/shard_map/ppermute | solution.py:53
  242.2 19.3 %collective-permute-done.26 = bf16[128,2048]{1,0:T(8,128)(2,1)S(1)} collective-permute-done((bf16[128,2048]{1,0:T(8,128)(2,1)S(1)}, bf16[128,2048]{1,0:T(8,128)(2,1)S(1)}, u32[]{:S(2)}, u32[]{:S(2)}) %collective-permute-start.26) | collective-permute-done | bytes 524320 | tf_op jit(solution)/shard_map/ppermute | solution.py:53
  373.6 19.3 %collective-permute-done.18 = bf16[128,2048]{1,0:T(8,128)(2,1)S(1)} collective-permute-done((bf16[128,2048]{1,0:T(8,128)(2,1)S(1)}, bf16[128,2048]{1,0:T(8,128)(2,1)S(1)}, u32[]{:S(2)}, u32[]{:S(2)}) %collective-permute-start.18) | collective-permute-done | bytes 524320 | tf_op jit(solution)/shard_map/ppermute | solution.py:53
  398.4 17.0 %collective-permute-done.36 = bf16[128,2048]{1,0:T(8,128)(2,1)S(1)} collective-permute-done((bf16[128,2048]{1,0:T(8,128)(2,1)S(1)}, bf16[128,2048]{1,0:T(8,128)(2,1)S(1)}, u32[]{:S(2)}, u32[]{:S(2)}) %collective-permute-start.36) | collective-permute-done | bytes 524320 | tf_op jit(solution)/shard_map/ppermute | solution.py:53
  420.8 17.0 %collective-permute-done.19 = bf16[128,2048]{1,0:T(8,128)(2,1)S(1)} collective-permute-done((bf16[128,2048]{1,0:T(8,128)(2,1)S(1)}, bf16[128,2048]{1,0:T(8,128)(2,1)S(1)}, u32[]{:S(2)}, u32[]{:S(2)}) %collective-permute-start.19) | collective-permute-done | bytes 524320 | tf_op jit(solution)/shard_map/ppermute | solution.py:53
  444.0 16.4 %collective-permute-done.37 = bf16[128,2048]{1,0:T(8,128)(2,1)S(1)} collective-permute-done((bf16[128,2048]{1,0:T(8,128)(2,1)S(1)}, bf16[128,2048]{1,0:T(8,128)(2,1)S(1)}, u32[]{:S(2)}, u32[]{:S(2)}) %collective-permute-start.37) | collective-permute-done | bytes 524320 | tf_op jit(solution)/shard_map/ppermute | solution.py:53
  466.4 15.7 %collective-permute-done.20 = bf16[128,2048]{1,0:T(8,128)(2,1)S(1)} collective-permute-done((bf16[128,2048]{1,0:T(8,128)(2,1)S(1)}, bf16[128,2048]{1,0:T(8,128)(2,1)S(1)}, u32[]{:S(2)}, u32[]{:S(2)}) %collective-permute-start.20) | collective-permute-done | bytes 524320 | tf_op jit(solution)/shard_map/ppermute | solution.py:53
  575.8 32.7 %all-gather.25.cloned.1.call-done = bf16[2048,2048]{1,0:T(8,128)(2,1)} async-done(((bf16[2048,256]{1,0:T(8,128)(2,1)}), bf16[2048,2048]{1,0:T(8,128)(2,1)}) %all-gather.25.cloned.1.call-update) | async-done | bytes 8388624 | tf_op jit(solution)/shard_map/all_gather | solution.py:160
  659.7 14.4 %convolution_bitcast_fusion.3 = bf16[2048,2048]{1,0:T(8,128)(2,1)} fusion(bf16[4,128,2048]{2,1,0:T(8,128)(2,1)} %get-tuple-element.189, bf16[4,128,2048]{2,1,0:T(8,128)(2,1)} %get-tuple-element.187, bf16[1,256,2048]{2,1,0:T(8,128)(2,1)} %copy-done.45, bf16[1,256,2048]{2,1,0:T(8,128)(2,1)} %copy-done.46, bf16[1,256,2048]{2,1,0:T(8,128)(2,1)} %copy-done.47, ...), kind=kOutput, calls=%fused_computation.7 | convolution fusion | flops 8604614656 | bytes 16777216 | tf_op jit(solution)/shard_map/dot_general | solution.py:29
  804.9 18.6 %collective-permute-done.81 = bf16[128,2048]{1,0:T(8,128)(2,1)S(1)} collective-permute-done((bf16[128,2048]{1,0:T(8,128)(2,1)S(1)}, bf16[128,2048]{1,0:T(8,128)(2,1)S(1)}, u32[]{:S(2)}, u32[]{:S(2)}) %collective-permute-start.81) | collective-permute-done | bytes 524320 | tf_op jit(solution)/shard_map/ppermute | solution.py:40
  947.9 20.0 %collective-permute-start.68 = (bf16[128,2048]{1,0:T(8,128)(2,1)}, bf16[128,2048]{1,0:T(8,128)(2,1)}, u32[]{:S(2)}, u32[]{:S(2)}) collective-permute-start(bf16[128,2048]{1,0:T(8,128)(2,1)} %get-tuple-element.99), channel_id=1, source_target_pairs={{0,1},{1,2},{2,3},{4,5},{5,6},{6,7},{8,9},{9,10},{10,11},{12,13},{... | collective-permute-start | bytes 1572872 | tf_op jit(solution)/shard_map/ppermute | solution.py:53
  996.2 16.9 %collective-permute-done.86 = bf16[128,2048]{1,0:T(8,128)(2,1)S(1)} collective-permute-done((bf16[128,2048]{1,0:T(8,128)(2,1)S(1)}, bf16[128,2048]{1,0:T(8,128)(2,1)S(1)}, u32[]{:S(2)}, u32[]{:S(2)}) %collective-permute-start.86) | collective-permute-done | bytes 524320 | tf_op jit(solution)/shard_map/ppermute | solution.py:53
  1019.9 25.2 %collective-permute-start.96 = (bf16[128,2048]{1,0:T(8,128)(2,1)S(1)}, bf16[128,2048]{1,0:T(8,128)(2,1)S(1)}, u32[]{:S(2)}, u32[]{:S(2)}) collective-permute-start(bf16[128,2048]{1,0:T(8,128)(2,1)S(1)} %get-tuple-element.68), channel_id=1, source_target_pairs={{0,1},{1,2},{2,3},{4,5},{5,6},{6,7},{8,9},{9,10},{10,11},{12,13},{... | collective-permute-start | bytes 1572872 | tf_op jit(solution)/shard_map/ppermute | solution.py:39
  1189.1 17.9 %collective-permute-done.102 = bf16[256,2048]{1,0:T(8,128)(2,1)S(1)} collective-permute-done((bf16[256,2048]{1,0:T(8,128)(2,1)S(1)}, bf16[256,2048]{1,0:T(8,128)(2,1)S(1)}, u32[]{:S(2)}, u32[]{:S(2)}) %collective-permute-start.102) | collective-permute-done | bytes 1048608 | tf_op jit(solution)/shard_map/ppermute | solution.py:53
  1237.7 14.3 %collective-permute-done.103 = bf16[256,2048]{1,0:T(8,128)(2,1)} collective-permute-done((bf16[256,2048]{1,0:T(8,128)(2,1)}, bf16[256,2048]{1,0:T(8,128)(2,1)}, u32[]{:S(2)}, u32[]{:S(2)}) %collective-permute-start.103) | collective-permute-done | bytes 1048608 | tf_op jit(solution)/shard_map/ppermute | solution.py:53
  1321.9 19.2 %collective-permute-start.118 = (f32[3,2,2048]{2,0,1:T(4,128)S(1)}, f32[3,2,2048]{2,0,1:T(4,128)S(1)}, u32[]{:S(2)}, u32[]{:S(2)}) collective-permute-start(f32[3,2,2048]{2,0,1:T(4,128)S(1)} %add.569), channel_id=1, source_target_pairs={{0,2},{1,3},{2,0},{3,1},{4,6},{5,7},{6,4},{7,5},{8,10},{9,11},{10,... | collective-permute-start | bytes 147464 | tf_op jit(solution)/shard_map/ppermute | solution.py:116
  1344.0 20.7 %collective-permute-done.118 = f32[3,2,2048]{2,0,1:T(4,128)S(1)} collective-permute-done((f32[3,2,2048]{2,0,1:T(4,128)S(1)}, f32[3,2,2048]{2,0,1:T(4,128)S(1)}, u32[]{:S(2)}, u32[]{:S(2)}) %collective-permute-start.118) | collective-permute-done | bytes 49184 | tf_op jit(solution)/shard_map/ppermute | solution.py:116
  (782 shorter events, 898.8 us)
Async XLA Ops:
  7.2 99.4 %all-gather.11.cloned.1.call-start = ((), (), s32[]{:S(2)}) async-start(), calls=%async_computation.8 | async-start | bytes 7077888 | tf_op jit(solution)/shard_map/all_gather | solution.py:155
  11.6 112.8 %all-gather.13.cloned.1.call-start = ((), (), s32[]{:S(2)}) async-start(), calls=%async_computation.9 | async-start | bytes 2359296 | tf_op jit(solution)/shard_map/all_gather | solution.py:160
  12.4 310.2 %all-gather.19.cloned.1.call-start = ((), (), s32[]{:S(2)}) async-start(), calls=%async_computation.12 | async-start | bytes 2359296 | tf_op jit(solution)/shard_map/all_gather | solution.py:155
  13.2 325.2 %all-gather.17.cloned.1.call-start = ((), (), s32[]{:S(2)}) async-start(), calls=%async_computation.11 | async-start | bytes 5242880 | tf_op jit(solution)/shard_map/all_gather | solution.py:186
  13.8 324.6 %all-gather.15.cloned.1.call-start = ((), (), s32[]{:S(2)}) async-start(), calls=%async_computation.10 | async-start | bytes 9437184 | tf_op jit(solution)/shard_map/all_gather | solution.py:155
  16.5 346.2 %all-gather.21.cloned.1.call-start = ((), (), s32[]{:S(2)}) async-start(), calls=%async_computation.13 | async-start | bytes 2359296 | tf_op jit(solution)/shard_map/all_gather | solution.py:160
  18.4 507.8 %all-gather.27.cloned.1.call-start = ((), (), s32[]{:S(2)}) async-start(), calls=%async_computation.24 | async-start | bytes 5242880 | tf_op jit(solution)/shard_map/all_gather | solution.py:200
  19.2 544.7 %all-gather.23.cloned.1.call-start = ((), (), s32[]{:S(2)}) async-start(), calls=%async_computation.14 | async-start | bytes 9437184 | tf_op jit(solution)/shard_map/all_gather | solution.py:155
  20.4 588.1 %all-gather.25.cloned.1.call-start = ((), (), s32[]{:S(2)}) async-start(), calls=%async_computation.15 | async-start | bytes 9437184 | tf_op jit(solution)/shard_map/all_gather | solution.py:160
  152.6 44.7 %collective-permute-start.7 = (bf16[128,2048]{1,0:T(8,128)(2,1)S(1)}, bf16[128,2048]{1,0:T(8,128)(2,1)S(1)}, u32[]{:S(2)}, u32[]{:S(2)}) collective-permute-start(bf16[128,2048]{1,0:T(8,128)(2,1)S(1)} %get-tuple-element.139), channel_id=1, source_target_pairs={{0,1},{1,2},{4,5},{5,6},{8,9},{9,10},{12,13},{13,14},{16,17},{17,1... | collective-permute-start | bytes 1572872 | tf_op jit(solution)/shard_map/ppermute | solution.py:53
  279.0 839.9 %reduce-scatter.13.cloned.1.call-start = ((), (), s32[]{:S(2)}) async-start(), calls=%async_computation.18 | async-start | bytes 9437184 | tf_op jit(solution)/shard_map/reduce_scatter | solution.py:163
  538.9 86.1 %collective-permute-start.51 = (bf16[128,2048]{1,0:T(8,128)(2,1)}, bf16[128,2048]{1,0:T(8,128)(2,1)}, u32[]{:S(2)}, u32[]{:S(2)}) collective-permute-start(bf16[128,2048]{1,0:T(8,128)(2,1)} %collective-permute-done.50), channel_id=1, source_target_pairs={{1,0},{5,4},{9,8},{13,12},{17,16},{21,20},{25,24},{29,28}} | collective-permute-start | bytes 1572872 | tf_op jit(solution)/shard_map/ppermute | solution.py:40
  552.9 73.3 %collective-permute-start.53 = (bf16[128,2048]{1,0:T(8,128)(2,1)}, bf16[128,2048]{1,0:T(8,128)(2,1)}, u32[]{:S(2)}, u32[]{:S(2)}) collective-permute-start(bf16[128,2048]{1,0:T(8,128)(2,1)} %collective-permute-done.52), channel_id=1, source_target_pairs={{2,3},{6,7},{10,11},{14,15},{18,19},{22,23},{26,27},{30,31}} | collective-permute-start | bytes 1572872 | tf_op jit(solution)/shard_map/ppermute | solution.py:39
  659.7 462.1 %reduce-scatter.11.cloned.1.call-start = ((), (), s32[]{:S(2)}) async-start(), calls=%async_computation.17 | async-start | bytes 9437184 | tf_op jit(solution)/shard_map/reduce_scatter | solution.py:166
  674.2 541.5 %reduce-scatter.15.cloned.1.call-start = ((), (), s32[]{:S(2)}) async-start(), calls=%async_computation.19 | async-start | bytes 2359296 | tf_op jit(solution)/shard_map/reduce_scatter | solution.py:166
  829.3 388.2 %reduce-scatter.17.cloned.1.call-start = ((), (), s32[]{:S(2)}) async-start(), calls=%async_computation.20 | async-start | bytes 2359296 | tf_op jit(solution)/shard_map/reduce_scatter | solution.py:163
  872.6 389.6 %reduce-scatter.9.cloned.1.call-start = ((), (), s32[]{:S(2)}) async-start(), calls=%async_computation.16 | async-start | bytes 5242880 | tf_op jit(solution)/shard_map/reduce_scatter | solution.py:234
  893.2 371.6 %reduce-scatter.23.cloned.1.call-start = ((), (), s32[]{:S(2)}) async-start(), calls=%async_computation.23 | async-start | bytes 2359296 | tf_op jit(solution)/shard_map/reduce_scatter | solution.py:166
  932.9 46.7 %collective-permute-start.85 = (bf16[128,2048]{1,0:T(8,128)(2,1)}, bf16[128,2048]{1,0:T(8,128)(2,1)}, u32[]{:S(2)}, u32[]{:S(2)}) collective-permute-start(bf16[128,2048]{1,0:T(8,128)(2,1)} %get-tuple-element.113), channel_id=1, source_target_pairs={{0,1},{1,2},{4,5},{5,6},{8,9},{9,10},{12,13},{13,14},{16,17},{17,1... | collective-permute-start | bytes 1572872 | tf_op jit(solution)/shard_map/ppermute | solution.py:53
  947.9 46.2 %collective-permute-start.68 = (bf16[128,2048]{1,0:T(8,128)(2,1)}, bf16[128,2048]{1,0:T(8,128)(2,1)}, u32[]{:S(2)}, u32[]{:S(2)}) collective-permute-start(bf16[128,2048]{1,0:T(8,128)(2,1)} %get-tuple-element.99), channel_id=1, source_target_pairs={{0,1},{1,2},{2,3},{4,5},{5,6},{6,7},{8,9},{9,10},{10,11},{12,13},{... | collective-permute-start | bytes 1572872 | tf_op jit(solution)/shard_map/ppermute | solution.py:53
  1111.2 189.2 %reduce-scatter.19.cloned.1.call-start = ((), (), s32[]{:S(2)}) async-start(), calls=%async_computation.21 | async-start | bytes 9437184 | tf_op jit(solution)/shard_map/reduce_scatter | solution.py:163
  1111.8 256.9 %reduce-scatter.21.cloned.1.call-start = ((), (), s32[]{:S(2)}) async-start(), calls=%async_computation.22 | async-start | bytes 7077888 | tf_op jit(solution)/shard_map/reduce_scatter | solution.py:163
  1277.7 87.7 %collective-permute-start.110 = (bf16[128,4096]{1,0:T(8,128)(2,1)}, bf16[128,4096]{1,0:T(8,128)(2,1)}, u32[]{:S(2)}, u32[]{:S(2)}) collective-permute-start(bf16[128,4096]{1,0:T(8,128)(2,1)} %get-tuple-element.64), channel_id=1, source_target_pairs={{0,1},{1,2},{2,3},{4,5},{5,6},{6,7},{8,9},{9,10},{10,11},{12,13},{... | collective-permute-start | bytes 3145736 | tf_op jit(solution)/shard_map/ppermute | solution.py:53
  1318.8 46.6 %collective-permute-start.113 = (bf16[128,4096]{1,0:T(8,128)(2,1)}, bf16[128,4096]{1,0:T(8,128)(2,1)}, u32[]{:S(2)}, u32[]{:S(2)}) collective-permute-start(bf16[128,4096]{1,0:T(8,128)(2,1)} %add_convert_fusion), channel_id=1, source_target_pairs={{1,0},{2,1},{3,2},{5,4},{6,5},{7,6},{9,8},{10,9},{11,10},{13,12},{... | collective-permute-start | bytes 3145736 | tf_op jit(solution)/shard_map/ppermute | solution.py:54
  (252 other events, 6222.7 us)
Sparse Core Ops, SparseCore 0:
  11.7 48.1 all-gather.10
  62.3 28.0 all-gather.12
  92.9 27.7 all-gather.18
  122.2 140.3 all-gather.16
  264.8 56.8 all-gather.14
  323.5 28.0 all-gather.20
  353.2 138.1 all-gather.26
  493.9 56.2 all-gather.22
  552.6 55.8 all-gather.24
  659.8 71.4 reduce-scatter.12
  734.8 71.2 reduce-scatter.10
  829.4 46.3 reduce-scatter.14
  879.1 41.1 reduce-scatter.16
  922.4 120.6 reduce-scatter.8
  1111.3 42.6 reduce-scatter.22
  1157.3 71.3 reduce-scatter.18
  1231.9 61.7 reduce-scatter.20
where the time goes:
time: 1390 us; the launch traced here: 1380 us
  waiting for transfers between devices  580 us (42%)
  starting transfers between devices  322 us (23%)
  matrix products  290 us (21%)
  other arithmetic  112 us (8%)
  local copies, waits for them, and re-layouts  48 us (3%)
  between operations  25.5 us (2%)
    ppermute x30, waiting for transfers between devices, sink(): lax.ppermute(one.astype(BF), 'narrow', [(k, k + 1) for k in range(step)])  320 us
    ppermute x27, waiting for transfers between devices, spread(): lax.ppermute(down[-1], 'narrow', [(k, k - 1) for k in range(1, n - step +...  177 us
    ppermute x30, starting transfers between devices, sink(): lax.ppermute(one.astype(BF), 'narrow', [(k, k + 1) for k in range(step)])  142 us
    ppermute x27, starting transfers between devices, spread(): lax.ppermute(up[-1], 'narrow', [(k, k + 1) for k in range(step - 1, n - 1)])  86.5 us
    dot_general x12, matrix products, product(): lax.dot_general(left_side, right_side, (((left_side.ndim - 1,), (0,)), ((...  75.1 us
    dot_general x12, matrix products, right_inner(): lax.dot_general(left_side, right_side, (((left_side.ndim - 1,), (1,)), ((...  69.7 us
    dot_general x7, matrix products, left_inner(): lax.dot_general(left_side, right_side, ((rows, rows), ((), ())), preferre...  57.3 us
    ppermute x27, starting transfers between devices, spread(): lax.ppermute(down[-1], 'narrow', [(k, k - 1) for k in range(1, n - step +...  35.1 us
  transfers between devices with their start and end apart: 136, of which 51 were waited for; matrix products, arithmetic and copies ran while one was open for 29% of the time, Pallas kernels for 0%

commit v1 on v0

--- a/solution.py
+++ b/solution.py
@@ -2,6 +2,7 @@
 import jax.numpy as jnp
 from jax import lax
 from jax.sharding import PartitionSpec as P
+from jax.lax import axis_index, axis_size, ppermute
 
 HEAD_DIM = 128
 PIX = 256
@@ -157,7 +158,28 @@
         )
 
     def columns_of(piece):
-        return lax.all_gather(piece.astype(BF), "wide", axis=1, tiled=True)
+
+        def _lead_sums_all(target):
+            lower, earlier, view_out = (axis_size("wide"), axis_index("wide"), target.shape[1])
+            items = tuple(((tick, (tick + 1) % lower) for tick in range(lower)))
+            vals = tuple(((tick, (tick - 1) % lower) for tick in range(lower)))
+            near = jnp.zeros((*target.shape[:1], lower * view_out, *target.shape[2:]), target.dtype)
+            near = lax.dynamic_update_slice_in_dim(near, target, earlier * view_out, axis=1)
+            plain = state_next = target
+            t1 = lower // 2
+            for jj in range(1, t1 + 1):
+                plain = ppermute(plain, "wide", items)
+                near = lax.dynamic_update_slice_in_dim(
+                    near, plain, (earlier - jj) % lower * view_out, axis=1
+                )
+                if jj < lower - t1:
+                    state_next = ppermute(state_next, "wide", vals)
+                    near = lax.dynamic_update_slice_in_dim(
+                        near, state_next, (earlier + jj) % lower * view_out, axis=1
+                    )
+            return near
+
+        return _lead_sums_all(piece.astype(BF))
 
     def to_rows(g):
         return lax.psum_scatter(g.astype(BF), "wide", scatter_dimension=0, tiled=True).astype(F32)

time: 1390 us -> 1410 us (1.014)
  waiting for transfers between devices: 580 us -> 535 us
  starting transfers between devices: 322 us -> 355 us
  local copies, waits for them, and re-layouts: 48 us -> 76.4 us
    ppermute x30, waiting for transfers between devices: 320 us -> 188 us  [sink(): lax.ppermute(one.astype(BF), 'narrow', [(k, k + 1) for k in range(step)])]
    ppermute x0 -> x21, waiting for transfers between devices: none -> 62.2 us  [the longest x9 43.9 us: _lead_sums_all(): state_next = ppermute(state_next, 'wide', vals)]
    ppermute x27, waiting for transfers between devices: 177 us -> 233 us  [spread(): lax.ppermute(down[-1], 'narrow', [(k, k - 1) for k in range(1, n - step +...]
    all_gather x3 -> x0, waiting for transfers between devices: 32.8 us -> none  [columns_of(): return lax.all_gather(piece.astype(BF), 'wide', axis=1, tiled=True)]
    ppermute x0 -> x21, starting transfers between devices: none -> 25.9 us  [the longest x9 18.8 us: _lead_sums_all(): state_next = ppermute(state_next, 'wide', vals)]
    dynamic_update_slice x0 -> x21, local copies, waits for them, and re-layouts: none -> 23.2 us  [the longest x12 13.1 us: _lead_sums_all(): lax.dynamic_update_slice_in_dim(near, plain, (earlier - jj) % lower * vie...]
  transfers between devices with their start and end apart: 136 -> 154, of which waited for: 51 -> 59; matrix products, arithmetic and copies ran while one was open for 29% -> 31% of each run, Pallas kernels for 0% -> 0%
where the time goes in v1:
time: 1410 us; the launch traced here: 1400 us
  waiting for transfers between devices  535 us (38%)
  starting transfers between devices  355 us (25%)
  matrix products  285 us (20%)
  other arithmetic  120 us (9%)
  local copies, waits for them, and re-layouts  76.4 us (5%)
  between operations  26 us (2%)
    ppermute x27, waiting for transfers between devices, spread(): lax.ppermute(down[-1], 'narrow', [(k, k - 1) for k in range(1, n - step +...  233 us
    ppermute x30, waiting for transfers between devices, sink(): lax.ppermute(one.astype(BF), 'narrow', [(k, k + 1) for k in range(step)])  188 us
    ppermute x30, starting transfers between devices, sink(): lax.ppermute(one.astype(BF), 'narrow', [(k, k + 1) for k in range(step)])  146 us
    ppermute x27, starting transfers between devices, spread(): lax.ppermute(up[-1], 'narrow', [(k, k + 1) for k in range(step - 1, n - 1)])  89.4 us
    dot_general x12, matrix products, right_inner(): lax.dot_general(left_side, right_side, (((left_side.ndim - 1,), (1,)), ((...  70.2 us
    dot_general x12, matrix products, product(): lax.dot_general(left_side, right_side, (((left_side.ndim - 1,), (0,)), ((...  69.6 us
    dot_general x7, matrix products, left_inner(): lax.dot_general(left_side, right_side, ((rows, rows), ((), ())), preferre...  55.8 us
    ppermute x9, waiting for transfers between devices, _lead_sums_all(): state_next = ppermute(state_next, 'wide', vals)  43.9 us
  transfers between devices with their start and end apart: 154, of which 59 were waited for; matrix products, arithmetic and copies ran while one was open for 31% of the time, Pallas kernels for 0%

profile of v1, /device:TPU:0, one launch (start us, length us, event | category | flops | bytes accessed | tf_op | source)
XLA Modules:
  0.0 1397.4 jit_solution(8932732362972261087)
XLA Ops:
  87.4 19.5 %collective-permute-done.3 = bf16[256,2048]{1,0:T(8,128)(2,1)S(1)} collective-permute-done((bf16[256,2048]{1,0:T(8,128)(2,1)}, bf16[256,2048]{1,0:T(8,128)(2,1)S(1)}, u32[]{:S(2)}, u32[]{:S(2)}) %collective-permute-start.3) | collective-permute-done | bytes 1048608 | tf_op jit(solution)/shard_map/ppermute | solution.py:41
  108.0 10.9 fusion.91
  138.8 20.7 %collective-permute-done.13 = bf16[128,2048]{1,0:T(8,128)(2,1)S(1)} collective-permute-done((bf16[128,2048]{1,0:T(8,128)(2,1)S(1)}, bf16[128,2048]{1,0:T(8,128)(2,1)S(1)}, u32[]{:S(2)}, u32[]{:S(2)}) %collective-permute-start.13) | collective-permute-done | bytes 524320 | tf_op jit(solution)/shard_map/ppermute | solution.py:54
  167.6 14.4 %collective-permute-done.38 = bf16[128,2048]{1,0:T(8,128)(2,1)S(1)} collective-permute-done((bf16[128,2048]{1,0:T(8,128)(2,1)S(1)}, bf16[128,2048]{1,0:T(8,128)(2,1)S(1)}, u32[]{:S(2)}, u32[]{:S(2)}) %collective-permute-start.38) | collective-permute-done | bytes 524320 | tf_op jit(solution)/shard_map/ppermute | solution.py:54
  210.6 12.3 collective-permute-done.39
  252.4 38.2 %collective-permute-done.28 = bf16[512,256]{1,0:T(8,128)(2,1)S(1)} collective-permute-done((bf16[512,256]{1,0:T(8,128)(2,1)S(1)}, bf16[512,256]{1,0:T(8,128)(2,1)S(1)}, u32[]{:S(2)}, u32[]{:S(2)}) %collective-permute-start.28) | collective-permute-done | bytes 262176 | tf_op jit(solution)/shard_map/ppermute | solution.py:176
  325.1 22.0 %collective-permute-done.21 = bf16[128,2048]{1,0:T(8,128)(2,1)S(1)} collective-permute-done((bf16[128,2048]{1,0:T(8,128)(2,1)S(1)}, bf16[128,2048]{1,0:T(8,128)(2,1)S(1)}, u32[]{:S(2)}, u32[]{:S(2)}) %collective-permute-start.21) | collective-permute-done | bytes 524320 | tf_op jit(solution)/shard_map/ppermute | solution.py:41
  353.4 24.6 %collective-permute-done.46 = bf16[128,2048]{1,0:T(8,128)(2,1)S(1)} collective-permute-done((bf16[128,2048]{1,0:T(8,128)(2,1)S(1)}, bf16[128,2048]{1,0:T(8,128)(2,1)S(1)}, u32[]{:S(2)}, u32[]{:S(2)}) %collective-permute-start.46) | collective-permute-done | bytes 524320 | tf_op jit(solution)/shard_map/ppermute | solution.py:41
  380.1 38.9 %collective-permute-done.22 = bf16[128,2048]{1,0:T(8,128)(2,1)S(1)} collective-permute-done((bf16[128,2048]{1,0:T(8,128)(2,1)S(1)}, bf16[128,2048]{1,0:T(8,128)(2,1)S(1)}, u32[]{:S(2)}, u32[]{:S(2)}) %collective-permute-start.22) | collective-permute-done | bytes 524320 | tf_op jit(solution)/shard_map/ppermute | solution.py:41
  602.5 15.1 %collective-permute-done.59 = bf16[128,2048]{1,0:T(8,128)(2,1)S(1)} collective-permute-done((bf16[128,2048]{1,0:T(8,128)(2,1)}, bf16[128,2048]{1,0:T(8,128)(2,1)S(1)}, u32[]{:S(2)}, u32[]{:S(2)}) %collective-permute-start.59) | collective-permute-done | bytes 524320 | tf_op jit(solution)/shard_map/ppermute | solution.py:41
  666.9 12.2 convolution_bitcast_fusion.2
  679.1 14.3 %convolution_bitcast_fusion.3 = bf16[2048,2048]{1,0:T(8,128)(2,1)} fusion(bf16[4,128,2048]{2,1,0:T(8,128)(2,1)} %get-tuple-element.195, bf16[4,128,2048]{2,1,0:T(8,128)(2,1)} %get-tuple-element.193, bf16[1,256,2048]{2,1,0:T(8,128)(2,1)} %copy-done.45, bf16[1,256,2048]{2,1,0:T(8,128)(2,1)} %copy-done.46, bf16[1,256,2048]{2,1,0:T(8,128)(2,1)} %copy-done.47, ...), kind=kOutput, calls=%fused_computation.7 | convolution fusion | flops 8604614656 | bytes 16777216 | tf_op jit(solution)/shard_map/dot_general | solution.py:30
  824.8 18.9 %collective-permute-done.102 = bf16[128,2048]{1,0:T(8,128)(2,1)S(1)} collective-permute-done((bf16[128,2048]{1,0:T(8,128)(2,1)S(1)}, bf16[128,2048]{1,0:T(8,128)(2,1)S(1)}, u32[]{:S(2)}, u32[]{:S(2)}) %collective-permute-start.102) | collective-permute-done | bytes 524320 | tf_op jit(solution)/shard_map/ppermute | solution.py:41
  949.2 12.8 collective-permute-start.106
  966.3 13.3 collective-permute-start.89
  993.3 15.2 %collective-permute-start.107 = (bf16[128,2048]{1,0:T(8,128)(2,1)S(1)}, bf16[128,2048]{1,0:T(8,128)(2,1)S(1)}, u32[]{:S(2)}, u32[]{:S(2)}) collective-permute-start(bf16[128,2048]{1,0:T(8,128)(2,1)S(1)} %get-tuple-element.117), channel_id=1, source_target_pairs={{0,1},{1,2},{2,3},{4,5},{5,6},{6,7},{8,9},{9,10},{10,11},{12,13},{... | collective-permute-start | bytes 1572872 | tf_op jit(solution)/shard_map/ppermute | solution.py:54
  1011.9 16.2 %collective-permute-done.107 = bf16[128,2048]{1,0:T(8,128)(2,1)S(1)} collective-permute-done((bf16[128,2048]{1,0:T(8,128)(2,1)S(1)}, bf16[128,2048]{1,0:T(8,128)(2,1)S(1)}, u32[]{:S(2)}, u32[]{:S(2)}) %collective-permute-start.107) | collective-permute-done | bytes 524320 | tf_op jit(solution)/shard_map/ppermute | solution.py:54
  1034.8 30.0 %collective-permute-start.117 = (bf16[128,2048]{1,0:T(8,128)(2,1)S(1)}, bf16[128,2048]{1,0:T(8,128)(2,1)S(1)}, u32[]{:S(2)}, u32[]{:S(2)}) collective-permute-start(bf16[128,2048]{1,0:T(8,128)(2,1)S(1)} %get-tuple-element.68), channel_id=1, source_target_pairs={{0,1},{1,2},{2,3},{4,5},{5,6},{6,7},{8,9},{9,10},{10,11},{12,13},{... | collective-permute-start | bytes 1572872 | tf_op jit(solution)/shard_map/ppermute | solution.py:40
  1190.0 10.8 fusion.94
  1208.6 18.1 %collective-permute-done.123 = bf16[256,2048]{1,0:T(8,128)(2,1)S(1)} collective-permute-done((bf16[256,2048]{1,0:T(8,128)(2,1)S(1)}, bf16[256,2048]{1,0:T(8,128)(2,1)S(1)}, u32[]{:S(2)}, u32[]{:S(2)}) %collective-permute-start.123) | collective-permute-done | bytes 1048608 | tf_op jit(solution)/shard_map/ppermute | solution.py:54
  1257.4 14.3 %collective-permute-done.124 = bf16[256,2048]{1,0:T(8,128)(2,1)} collective-permute-done((bf16[256,2048]{1,0:T(8,128)(2,1)}, bf16[256,2048]{1,0:T(8,128)(2,1)}, u32[]{:S(2)}, u32[]{:S(2)}) %collective-permute-start.124) | collective-permute-done | bytes 1048608 | tf_op jit(solution)/shard_map/ppermute | solution.py:54
  1304.4 12.2 collective-permute-done.125
  1341.6 19.2 %collective-permute-start.139 = (f32[3,2,2048]{2,0,1:T(4,128)S(1)}, f32[3,2,2048]{2,0,1:T(4,128)S(1)}, u32[]{:S(2)}, u32[]{:S(2)}) collective-permute-start(f32[3,2,2048]{2,0,1:T(4,128)S(1)} %add.682), channel_id=1, source_target_pairs={{0,2},{1,3},{2,0},{3,1},{4,6},{5,7},{6,4},{7,5},{8,10},{9,11},{10,... | collective-permute-start | bytes 147464 | tf_op jit(solution)/shard_map/ppermute | solution.py:117
  1363.6 20.7 %collective-permute-done.139 = f32[3,2,2048]{2,0,1:T(4,128)S(1)} collective-permute-done((f32[3,2,2048]{2,0,1:T(4,128)S(1)}, f32[3,2,2048]{2,0,1:T(4,128)S(1)}, u32[]{:S(2)}, u32[]{:S(2)}) %collective-permute-start.139) | collective-permute-done | bytes 49184 | tf_op jit(solution)/shard_map/ppermute | solution.py:117
  (827 shorter events, 926.6 us)
Async XLA Ops:
  7.2 100.8 %all-gather.8.cloned.1.call-start = ((), (), s32[]{:S(2)}) async-start(), calls=%async_computation.8 | async-start | bytes 7077888 | tf_op jit(solution)/shard_map/all_gather | solution.py:156
  11.6 420.8 %all-gather.14.cloned.1.call-start = ((), (), s32[]{:S(2)}) async-start(), calls=%async_computation.11 | async-start | bytes 2359296 | tf_op jit(solution)/shard_map/all_gather | solution.py:156
  12.4 430.9 %all-gather.12.cloned.1.call-start = ((), (), s32[]{:S(2)}) async-start(), calls=%async_computation.10 | async-start | bytes 5242880 | tf_op jit(solution)/shard_map/all_gather | solution.py:208
  13.2 430.2 %all-gather.10.cloned.1.call-start = ((), (), s32[]{:S(2)}) async-start(), calls=%async_computation.9 | async-start | bytes 9437184 | tf_op jit(solution)/shard_map/all_gather | solution.py:156
  14.6 559.5 %all-gather.18.cloned.1.call-start = ((), (), s32[]{:S(2)}) async-start(), calls=%async_computation.21 | async-start | bytes 5242880 | tf_op jit(solution)/shard_map/all_gather | solution.py:222
  15.1 605.3 %all-gather.16.cloned.1.call-start = ((), (), s32[]{:S(2)}) async-start(), calls=%async_computation.12 | async-start | bytes 9437184 | tf_op jit(solution)/shard_map/all_gather | solution.py:156
  32.2 198.9 %collective-permute-start.25 = (bf16[512,256]{1,0:T(8,128)(2,1)}, bf16[512,256]{1,0:T(8,128)(2,1)}, u32[]{:S(2)}, u32[]{:S(2)}) collective-permute-start(bf16[512,256]{1,0:T(8,128)(2,1)} %get-tuple-element.85), channel_id=1, source_target_pairs={{0,4},{4,8},{8,12},{12,16},{16,20},{20,24},{24,28},{28,0},{1,5},{5... | collective-permute-start | bytes 786440 | tf_op jit(solution)/shard_map/ppermute | solution.py:171
  35.0 1103.7 %reduce-scatter.13.cloned.1.call-start = ((), (), s32[]{:S(2)}) async-start(), calls=%async_computation.15 | async-start | bytes 9437184 | tf_op jit(solution)/shard_map/reduce_scatter | solution.py:185
  239.4 64.8 %collective-permute-start.62 = (bf16[2048,256]{1,0:T(8,128)(2,1)}, bf16[2048,256]{1,0:T(8,128)(2,1)}, u32[]{:S(2)}, u32[]{:S(2)}) collective-permute-start(bf16[2048,256]{1,0:T(8,128)(2,1)} %get-tuple-element.77), channel_id=1, source_target_pairs={{0,4},{4,8},{8,12},{12,16},{16,20},{20,24},{24,28},{28,0},{1,5},{5... | collective-permute-start | bytes 3145736 | tf_op jit(solution)/shard_map/ppermute | solution.py:171
  239.4 70.2 %collective-permute-start.63 = (bf16[2048,256]{1,0:T(8,128)(2,1)}, bf16[2048,256]{1,0:T(8,128)(2,1)}, u32[]{:S(2)}, u32[]{:S(2)}) collective-permute-start(bf16[2048,256]{1,0:T(8,128)(2,1)} %get-tuple-element.77), channel_id=1, source_target_pairs={{0,28},{4,0},{8,4},{12,8},{16,12},{20,16},{24,20},{28,24},{1,29},{... | collective-permute-start | bytes 3145736 | tf_op jit(solution)/shard_map/ppermute | solution.py:176
  251.1 60.3 %collective-permute-start.20 = (bf16[128,2048]{1,0:T(8,128)(2,1)S(1)}, bf16[128,2048]{1,0:T(8,128)(2,1)S(1)}, u32[]{:S(2)}, u32[]{:S(2)}) collective-permute-start(bf16[128,2048]{1,0:T(8,128)(2,1)S(1)} %get-tuple-element.174), channel_id=1, source_target_pairs={{1,0},{2,1},{3,2},{5,4},{6,5},{7,6},{9,8},{10,9},{11,10},{13,12},{... | collective-permute-start | bytes 1572872 | tf_op jit(solution)/shard_map/ppermute | solution.py:41
  318.2 169.7 %collective-permute-start.64 = (bf16[2048,256]{1,0:T(8,128)(2,1)}, bf16[2048,256]{1,0:T(8,128)(2,1)}, u32[]{:S(2)}, u32[]{:S(2)}) collective-permute-start(bf16[2048,256]{1,0:T(8,128)(2,1)} %collective-permute-done.62), channel_id=1, source_target_pairs={{0,4},{4,8},{8,12},{12,16},{16,20},{20,24},{24,28},{28,0},{1,5},{5... | collective-permute-start | bytes 3145736 | tf_op jit(solution)/shard_map/ppermute | solution.py:171
  318.3 59.7 %collective-permute-start.46 = (bf16[128,2048]{1,0:T(8,128)(2,1)S(1)}, bf16[128,2048]{1,0:T(8,128)(2,1)S(1)}, u32[]{:S(2)}, u32[]{:S(2)}) collective-permute-start(bf16[128,2048]{1,0:T(8,128)(2,1)S(1)} %collective-permute-done.45), channel_id=1, source_target_pairs={{1,0},{2,1},{5,4},{6,5},{9,8},{10,9},{13,12},{14,13},{17,16},{18,1... | collective-permute-start | bytes 1572872 | tf_op jit(solution)/shard_map/ppermute | solution.py:41
  347.1 167.2 %collective-permute-start.65 = (bf16[2048,256]{1,0:T(8,128)(2,1)}, bf16[2048,256]{1,0:T(8,128)(2,1)}, u32[]{:S(2)}, u32[]{:S(2)}) collective-permute-start(bf16[2048,256]{1,0:T(8,128)(2,1)} %collective-permute-done.63), channel_id=1, source_target_pairs={{0,28},{4,0},{8,4},{12,8},{16,12},{20,16},{24,20},{28,24},{1,29},{... | collective-permute-start | bytes 3145736 | tf_op jit(solution)/shard_map/ppermute | solution.py:176
  352.1 67.0 %collective-permute-start.22 = (bf16[128,2048]{1,0:T(8,128)(2,1)S(1)}, bf16[128,2048]{1,0:T(8,128)(2,1)S(1)}, u32[]{:S(2)}, u32[]{:S(2)}) collective-permute-start(bf16[128,2048]{1,0:T(8,128)(2,1)S(1)} %collective-permute-done.21), channel_id=1, source_target_pairs={{1,0},{5,4},{9,8},{13,12},{17,16},{21,20},{25,24},{29,28}} | collective-permute-start | bytes 1572872 | tf_op jit(solution)/shard_map/ppermute | solution.py:41
  583.9 62.6 %collective-permute-start.72 = (bf16[128,2048]{1,0:T(8,128)(2,1)}, bf16[128,2048]{1,0:T(8,128)(2,1)}, u32[]{:S(2)}, u32[]{:S(2)}) collective-permute-start(bf16[128,2048]{1,0:T(8,128)(2,1)} %collective-permute-done.71), channel_id=1, source_target_pairs={{1,0},{5,4},{9,8},{13,12},{17,16},{21,20},{25,24},{29,28}} | collective-permute-start | bytes 1572872 | tf_op jit(solution)/shard_map/ppermute | solution.py:41
  679.0 462.5 %reduce-scatter.11.cloned.1.call-start = ((), (), s32[]{:S(2)}) async-start(), calls=%async_computation.14 | async-start | bytes 9437184 | tf_op jit(solution)/shard_map/reduce_scatter | solution.py:188
  693.5 542.0 %reduce-scatter.15.cloned.1.call-start = ((), (), s32[]{:S(2)}) async-start(), calls=%async_computation.16 | async-start | bytes 2359296 | tf_op jit(solution)/shard_map/reduce_scatter | solution.py:188
  849.0 388.2 %reduce-scatter.17.cloned.1.call-start = ((), (), s32[]{:S(2)}) async-start(), calls=%async_computation.17 | async-start | bytes 2359296 | tf_op jit(solution)/shard_map/reduce_scatter | solution.py:185
  889.7 392.2 %reduce-scatter.9.cloned.1.call-start = ((), (), s32[]{:S(2)}) async-start(), calls=%async_computation.13 | async-start | bytes 5242880 | tf_op jit(solution)/shard_map/reduce_scatter | solution.py:256
  909.8 374.7 %reduce-scatter.23.cloned.1.call-start = ((), (), s32[]{:S(2)}) async-start(), calls=%async_computation.20 | async-start | bytes 2359296 | tf_op jit(solution)/shard_map/reduce_scatter | solution.py:188
  1131.2 188.9 %reduce-scatter.19.cloned.1.call-start = ((), (), s32[]{:S(2)}) async-start(), calls=%async_computation.18 | async-start | bytes 9437184 | tf_op jit(solution)/shard_map/reduce_scatter | solution.py:185
  1131.9 256.4 %reduce-scatter.21.cloned.1.call-start = ((), (), s32[]{:S(2)}) async-start(), calls=%async_computation.19 | async-start | bytes 7077888 | tf_op jit(solution)/shard_map/reduce_scatter | solution.py:185
  1297.3 87.7 %collective-permute-start.131 = (bf16[128,4096]{1,0:T(8,128)(2,1)}, bf16[128,4096]{1,0:T(8,128)(2,1)}, u32[]{:S(2)}, u32[]{:S(2)}) collective-permute-start(bf16[128,4096]{1,0:T(8,128)(2,1)} %get-tuple-element.64), channel_id=1, source_target_pairs={{0,1},{1,2},{2,3},{4,5},{5,6},{6,7},{8,9},{9,10},{10,11},{12,13},{... | collective-permute-start | bytes 3145736 | tf_op jit(solution)/shard_map/ppermute | solution.py:54
  (264 other events, 7116.3 us)
Sparse Core Ops, SparseCore 0:
  11.7 55.6 all-gather.7
  69.4 29.1 all-gather.13
  100.2 118.6 all-gather.11
  220.6 84.7 all-gather.9
  306.8 113.3 all-gather.17
  421.9 52.3 all-gather.15
  679.2 76.1 reduce-scatter.12
  758.9 71.2 reduce-scatter.10
  849.2 47.8 reduce-scatter.14
  900.2 41.0 reduce-scatter.16
  943.6 116.5 reduce-scatter.8
  1131.3 42.5 reduce-scatter.22
  1177.3 71.3 reduce-scatter.18
  1252.0 61.7 reduce-scatter.20
